TPU v7x, 32 devices: a whole 2x2x4 slice. The times are simulated.
32 devices in a mesh: ctx: 8 (over z, y), head: 4 (over x, core).
Axes of the slice: x: 2, y: 2, z: 4, core: 2. Of those that a mesh axis runs over, the one named last changes fastest.
Arguments:
- queries: bfloat16 [2048, 8192], P('ctx', 'head'), may hold values from -15 to 15
- keys: bfloat16 [2048, 1024], P('ctx'), may hold values from -6 to 6
- values: bfloat16 [2048, 1024], P('ctx'), may hold values from -6 to 6
Outputs:
- attended: bfloat16 [2048, 8192], P('ctx', 'head')
All inputs are finite; a program needn't handle non-finite values.
Results may differ from a plain program's by a relative error of at most 0.015.
Values may be sent and summed in bfloat16 or wider, within the bound.
No kernel may reach another device: no remote copies, remote signals or barrier semaphores. Data moves between devices by JAX's collectives and lax.ppermute only.
A program may use at most 128 MiB of HBM per device.

v0:
```python
import jax
import jax.numpy as jnp
from jax import lax
from jax.sharding import PartitionSpec as P

H = 64
KVH = 8
HD = 128


negative_big = -1e30


def shifted(value, axis, steps):
    count = lax.axis_size(axis)
    initial, last = (max(0, -steps), min(count, count - steps))
    return lax.ppermute(value, axis, [(source, source + steps) for source in range(initial, last)])


def attend(acc_state, grouped, key_piece, value_piece, allowed):
    maxima, totals, running_sum = acc_state
    scores = jnp.einsum(
        "qgrd,kgd->grqk", grouped, key_piece, preferred_element_type=jnp.float32
    ) * HD ** (-0.5)
    scores = jnp.where(allowed, scores, negative_big)
    new_max = jnp.maximum(maxima, jnp.max(scores, axis=-1))
    weights = jnp.where(allowed, jnp.exp(scores - new_max[..., None]), 0.0)
    factor = jnp.exp(maxima - new_max)
    totals = totals * factor + jnp.sum(weights, axis=-1)
    running_sum = running_sum * factor[..., None] + jnp.einsum(
        "grqk,kgd->grqd",
        weights.astype(jnp.bfloat16),
        value_piece,
        preferred_element_type=jnp.float32,
    )
    return (new_max, totals, running_sum)


def keep_state(carried):
    return carried


def circulate(acc_state, grouped, kv_pair, ctx_place, turn_limit, full_mask):

    def cycle_turn(turn_index, carried):
        acc_now, pieces = carried
        pieces = shifted(pieces, "ctx", 1)
        acc_now = lax.cond(
            ctx_place >= turn_index,
            lambda held: attend(held, grouped, pieces[0], pieces[1], full_mask),
            keep_state,
            acc_now,
        )
        return (acc_now, pieces)

    acc_state, kv_pair = lax.fori_loop(1, turn_limit, cycle_turn, (acc_state, kv_pair))
    return acc_state


def body(queries, keys, values):
    tok_rows = queries.shape[0]
    heads_dev = queries.shape[1] // HD
    group_size = H // KVH
    kv_count = max(1, heads_dev // group_size)
    repeat = heads_dev // kv_count
    grouped = queries.reshape(tok_rows, kv_count, repeat, HD)
    first_col = lax.axis_index("head") * heads_dev // group_size * HD
    keys_flat = lax.dynamic_slice_in_dim(keys, first_col, kv_count * HD, 1)
    values_flat = lax.dynamic_slice_in_dim(values, first_col, kv_count * HD, 1)
    keys_used = keys_flat.reshape(tok_rows, kv_count, HD)
    values_used = values_flat.reshape(tok_rows, kv_count, HD)
    ctx_count = lax.axis_size("ctx")
    ctx_place = lax.axis_index("ctx")
    positions = jnp.arange(tok_rows, dtype=jnp.int32)
    causal_mask = positions[:, None] >= positions[None, :]
    full_mask = jnp.ones((tok_rows, tok_rows), bool)
    blank_state = (
        jnp.full((kv_count, repeat, tok_rows), negative_big, jnp.float32),
        jnp.zeros((kv_count, repeat, tok_rows), jnp.float32),
        jnp.zeros((kv_count, repeat, tok_rows, HD), jnp.float32),
    )
    kv_pair = jnp.stack([keys_used, values_used])
    acc_state = attend(blank_state, grouped, keys_used, values_used, causal_mask)
    acc_state = circulate(acc_state, grouped, kv_pair, ctx_place, ctx_count, full_mask)
    result = acc_state[2] / acc_state[1][..., None]
    return (
        jnp.transpose(result, (2, 0, 1, 3)).reshape(tok_rows, heads_dev * HD).astype(jnp.bfloat16)
    )


def solution(mesh):
    return jax.shard_map(
        body,
        mesh=mesh,
        in_specs=(P("ctx", "head"), P("ctx", None), P("ctx", None)),
        out_specs=P("ctx", "head"),
        check_vma=False,
    )
```

profile of v0, /device:TPU:30, one launch (start us, length us, event | category | flops | bytes accessed | tf_op | source)
XLA Modules:
  0.0 107.5 jit_solution(7693095241072445653)
XLA Ops:
  1.2 1.5 %copy.9 = bf16[256,2048]{0,1:T(8,128)(2,1)S(1)} copy(bf16[256,2048]{1,0:T(8,128)(2,1)} %param.7) | data formatting | bytes 2097152 | tf_op args[0]
  3.5 1.9 %copy-done = f32[2,256,256,8]{2,1,3,0:T(8,128)} copy-done((f32[2,256,256,8]{2,1,3,0:T(8,128)}, f32[2,256,256,8]{2,1,3,0:T(8,128)S(1)}, u32[]{:S(2)}) %copy-start) | copy-done | bytes 4194328
  6.6 3.4 %fusion.25 = f32[2,8,256,128]{3,2,1,0:T(8,128)S(1)} fusion(bf16[256,2,128,1]{0,2,3,1:T(8,128)(2,1)S(1)} %bitcast.68, f32[2,256,256,8]{2,1,3,0:T(8,128)} %copy-done, f32[2,8,256]{2,1,0:T(8,128)S(1)} %broadcast_maximum_fusion, pred[256,256]{0,1:T(8,128)(4,1)S(1)} %iota_compare_fusion, f32[2,8,256]{2,1,0:T(8,128)S(1)} %get-tuple-element.187), kind=kOutput, calls=%fused_computation.29 | convolution fusion | flops 274202624 | bytes 6520832 | tf_op jit(solution)/shard_map/grqk,kgd->grqd/dot_general | solution.py:30
  10.9 1.6 %copy.16 = bf16[256,2,8,128]{3,0,2,1:T(8,128)(2,1)S(1)} copy(bf16[256,2,8,128]{0,3,2,1:T(8,128)(2,1)} %bitcast.64) | data formatting | bytes 2097152 | tf_op jit(solution)/shard_map/while | solution.py:56
  12.5 92.4 %while.19 = (s32[]{:T(128)}, f32[2,8,256]{2,1,0:T(8,128)S(1)}, f32[2,8,256]{2,1,0:T(8,128)S(1)}, f32[2,8,256,128]{3,2,1,0:T(8,128)S(1)}, bf16[2,256,2,128]{3,1,2...) while((s32[]{:T(128)}, f32[2,8,256]{2,1,0:T(8,128)S(1)}, ...), condition=%wide.region_7.8_spmd, body=%wide.region_2.7_spmd.sunk | while | flops 546316288 | bytes 19923180 | solution.py:56
  12.5 1.3 %collective-permute-start = (bf16[2,256,2,128]{3,1,2,0:T(8,128)(2,1)}, bf16[2,256,2,128]{3,1,2,0:T(8,128)(2,1)S(1)}, u32[]{:S(2)}, u32[]{:S(2)}) collective-permute-start(bf16[2,256,2,128]{3,1,2,0:T(8,128)(2,1)} %get-tuple-element.260), channel_id=1, source_target_pairs={{0,4},{4,8},{8,12},{12,16},{16,20},{20,24},{24,28},{1,5},{5,9},{9,... | collective-permute-start | bytes 786440 | tf_op jit(solution)/shard_map/while/body/eval_jaxpr/ppermute | solution.py:17
  13.8 8.8 %collective-permute-done = bf16[2,256,2,128]{3,1,2,0:T(8,128)(2,1)S(1)} collective-permute-done((bf16[2,256,2,128]{3,1,2,0:T(8,128)(2,1)}, bf16[2,256,2,128]{3,1,2,0:T(8,128)(2,1)S(1)}, u32[]{:S(2)}, u32[]{:S(2)}) %collective-permute-start) | collective-permute-done | bytes 262176 | tf_op jit(solution)/shard_map/while/body/eval_jaxpr/ppermute | solution.py:17
  22.7 3.1 %conditional.2 = ((f32[2,8,256]{2,1,0:T(8,128)S(1)}, f32[2,8,256]{2,1,0:T(8,128)S(1)}, f32[2,8,256,128]{3,2,1,0:T(8,128)S(1)})) conditional(s32[]{:T(128)} %convert_element_type.38, (f32[2,8,256]{2,1,0:T(8,128)S(1)}, f32[2,8,256]{2,1,0:T(8,128)S(1)}, f32[2,8,256,128]{3,2,1,0:T(8,128)S(1)}) %tuple.43, (bf16[2,256,2,128]{3,1,2,0:T(8,128)(2,1)S(1)}, ...), branch_computations={%region_3.3_spmd, %region_4.6_spmd} | conditional | flops 546316288 | bytes 18350112 | solution.py:48
  24.1 1.6 %multiply_add_fusion = f32[2,8,256,128]{3,2,1,0:T(8,128)S(1)} fusion(f32[2,8,256,128]{3,2,1,0:T(8,128)S(1)} %get-tuple-element.146, f32[2,256,256,8]{2,1,3,0:T(8,128)S(1)} %get-tuple-element.186, f32[2,8,256]{2,1,0:T(8,128)S(1)} %max.2, f32[2,8,256]{2,1,0:T(8,128)S(1)} %get-tuple-element.184, bf16[2,256,2,128]{3,1,2,0:T(8,128)(2,1)S(1)} %get-tuple-element.143), kind=kOutput, calls=%fused_computation.6 | convolution fusion | flops 272629760 | bytes 8552448 | tf_op jit(solution)/shard_map/while/body/eval_jaxpr/cond/branch_1_fun/grqk,kgd->grqd/dot_general | solution.py:30
  26.5 1.3 %collective-permute-start = (bf16[2,256,2,128]{3,1,2,0:T(8,128)(2,1)}, bf16[2,256,2,128]{3,1,2,0:T(8,128)(2,1)S(1)}, u32[]{:S(2)}, u32[]{:S(2)}) collective-permute-start(bf16[2,256,2,128]{3,1,2,0:T(8,128)(2,1)} %get-tuple-element.260), channel_id=1, source_target_pairs={{0,4},{4,8},{8,12},{12,16},{16,20},{20,24},{24,28},{1,5},{5,9},{9,... | collective-permute-start | bytes 786440 | tf_op jit(solution)/shard_map/while/body/eval_jaxpr/ppermute | solution.py:17
  27.8 8.0 %collective-permute-done = bf16[2,256,2,128]{3,1,2,0:T(8,128)(2,1)S(1)} collective-permute-done((bf16[2,256,2,128]{3,1,2,0:T(8,128)(2,1)}, bf16[2,256,2,128]{3,1,2,0:T(8,128)(2,1)S(1)}, u32[]{:S(2)}, u32[]{:S(2)}) %collective-permute-start) | collective-permute-done | bytes 262176 | tf_op jit(solution)/shard_map/while/body/eval_jaxpr/ppermute | solution.py:17
  35.8 3.1 %conditional.2 = ((f32[2,8,256]{2,1,0:T(8,128)S(1)}, f32[2,8,256]{2,1,0:T(8,128)S(1)}, f32[2,8,256,128]{3,2,1,0:T(8,128)S(1)})) conditional(s32[]{:T(128)} %convert_element_type.38, (f32[2,8,256]{2,1,0:T(8,128)S(1)}, f32[2,8,256]{2,1,0:T(8,128)S(1)}, f32[2,8,256,128]{3,2,1,0:T(8,128)S(1)}) %tuple.43, (bf16[2,256,2,128]{3,1,2,0:T(8,128)(2,1)S(1)}, ...), branch_computations={%region_3.3_spmd, %region_4.6_spmd} | conditional | flops 546316288 | bytes 18350112 | solution.py:48
  37.3 1.6 %multiply_add_fusion = f32[2,8,256,128]{3,2,1,0:T(8,128)S(1)} fusion(f32[2,8,256,128]{3,2,1,0:T(8,128)S(1)} %get-tuple-element.146, f32[2,256,256,8]{2,1,3,0:T(8,128)S(1)} %get-tuple-element.186, f32[2,8,256]{2,1,0:T(8,128)S(1)} %max.2, f32[2,8,256]{2,1,0:T(8,128)S(1)} %get-tuple-element.184, bf16[2,256,2,128]{3,1,2,0:T(8,128)(2,1)S(1)} %get-tuple-element.143), kind=kOutput, calls=%fused_computation.6 | convolution fusion | flops 272629760 | bytes 8552448 | tf_op jit(solution)/shard_map/while/body/eval_jaxpr/cond/branch_1_fun/grqk,kgd->grqd/dot_general | solution.py:30
  39.6 1.3 %collective-permute-start = (bf16[2,256,2,128]{3,1,2,0:T(8,128)(2,1)}, bf16[2,256,2,128]{3,1,2,0:T(8,128)(2,1)S(1)}, u32[]{:S(2)}, u32[]{:S(2)}) collective-permute-start(bf16[2,256,2,128]{3,1,2,0:T(8,128)(2,1)} %get-tuple-element.260), channel_id=1, source_target_pairs={{0,4},{4,8},{8,12},{12,16},{16,20},{20,24},{24,28},{1,5},{5,9},{9,... | collective-permute-start | bytes 786440 | tf_op jit(solution)/shard_map/while/body/eval_jaxpr/ppermute | solution.py:17
  40.9 7.7 %collective-permute-done = bf16[2,256,2,128]{3,1,2,0:T(8,128)(2,1)S(1)} collective-permute-done((bf16[2,256,2,128]{3,1,2,0:T(8,128)(2,1)}, bf16[2,256,2,128]{3,1,2,0:T(8,128)(2,1)S(1)}, u32[]{:S(2)}, u32[]{:S(2)}) %collective-permute-start) | collective-permute-done | bytes 262176 | tf_op jit(solution)/shard_map/while/body/eval_jaxpr/ppermute | solution.py:17
  48.6 3.1 %conditional.2 = ((f32[2,8,256]{2,1,0:T(8,128)S(1)}, f32[2,8,256]{2,1,0:T(8,128)S(1)}, f32[2,8,256,128]{3,2,1,0:T(8,128)S(1)})) conditional(s32[]{:T(128)} %convert_element_type.38, (f32[2,8,256]{2,1,0:T(8,128)S(1)}, f32[2,8,256]{2,1,0:T(8,128)S(1)}, f32[2,8,256,128]{3,2,1,0:T(8,128)S(1)}) %tuple.43, (bf16[2,256,2,128]{3,1,2,0:T(8,128)(2,1)S(1)}, ...), branch_computations={%region_3.3_spmd, %region_4.6_spmd} | conditional | flops 546316288 | bytes 18350112 | solution.py:48
  50.1 1.6 %multiply_add_fusion = f32[2,8,256,128]{3,2,1,0:T(8,128)S(1)} fusion(f32[2,8,256,128]{3,2,1,0:T(8,128)S(1)} %get-tuple-element.146, f32[2,256,256,8]{2,1,3,0:T(8,128)S(1)} %get-tuple-element.186, f32[2,8,256]{2,1,0:T(8,128)S(1)} %max.2, f32[2,8,256]{2,1,0:T(8,128)S(1)} %get-tuple-element.184, bf16[2,256,2,128]{3,1,2,0:T(8,128)(2,1)S(1)} %get-tuple-element.143), kind=kOutput, calls=%fused_computation.6 | convolution fusion | flops 272629760 | bytes 8552448 | tf_op jit(solution)/shard_map/while/body/eval_jaxpr/cond/branch_1_fun/grqk,kgd->grqd/dot_general | solution.py:30
  52.4 1.3 %collective-permute-start = (bf16[2,256,2,128]{3,1,2,0:T(8,128)(2,1)}, bf16[2,256,2,128]{3,1,2,0:T(8,128)(2,1)S(1)}, u32[]{:S(2)}, u32[]{:S(2)}) collective-permute-start(bf16[2,256,2,128]{3,1,2,0:T(8,128)(2,1)} %get-tuple-element.260), channel_id=1, source_target_pairs={{0,4},{4,8},{8,12},{12,16},{16,20},{20,24},{24,28},{1,5},{5,9},{9,... | collective-permute-start | bytes 786440 | tf_op jit(solution)/shard_map/while/body/eval_jaxpr/ppermute | solution.py:17
  53.7 7.8 %collective-permute-done = bf16[2,256,2,128]{3,1,2,0:T(8,128)(2,1)S(1)} collective-permute-done((bf16[2,256,2,128]{3,1,2,0:T(8,128)(2,1)}, bf16[2,256,2,128]{3,1,2,0:T(8,128)(2,1)S(1)}, u32[]{:S(2)}, u32[]{:S(2)}) %collective-permute-start) | collective-permute-done | bytes 262176 | tf_op jit(solution)/shard_map/while/body/eval_jaxpr/ppermute | solution.py:17
  61.5 3.1 %conditional.2 = ((f32[2,8,256]{2,1,0:T(8,128)S(1)}, f32[2,8,256]{2,1,0:T(8,128)S(1)}, f32[2,8,256,128]{3,2,1,0:T(8,128)S(1)})) conditional(s32[]{:T(128)} %convert_element_type.38, (f32[2,8,256]{2,1,0:T(8,128)S(1)}, f32[2,8,256]{2,1,0:T(8,128)S(1)}, f32[2,8,256,128]{3,2,1,0:T(8,128)S(1)}) %tuple.43, (bf16[2,256,2,128]{3,1,2,0:T(8,128)(2,1)S(1)}, ...), branch_computations={%region_3.3_spmd, %region_4.6_spmd} | conditional | flops 546316288 | bytes 18350112 | solution.py:48
  63.0 1.6 %multiply_add_fusion = f32[2,8,256,128]{3,2,1,0:T(8,128)S(1)} fusion(f32[2,8,256,128]{3,2,1,0:T(8,128)S(1)} %get-tuple-element.146, f32[2,256,256,8]{2,1,3,0:T(8,128)S(1)} %get-tuple-element.186, f32[2,8,256]{2,1,0:T(8,128)S(1)} %max.2, f32[2,8,256]{2,1,0:T(8,128)S(1)} %get-tuple-element.184, bf16[2,256,2,128]{3,1,2,0:T(8,128)(2,1)S(1)} %get-tuple-element.143), kind=kOutput, calls=%fused_computation.6 | convolution fusion | flops 272629760 | bytes 8552448 | tf_op jit(solution)/shard_map/while/body/eval_jaxpr/cond/branch_1_fun/grqk,kgd->grqd/dot_general | solution.py:30
  65.3 1.3 %collective-permute-start = (bf16[2,256,2,128]{3,1,2,0:T(8,128)(2,1)}, bf16[2,256,2,128]{3,1,2,0:T(8,128)(2,1)S(1)}, u32[]{:S(2)}, u32[]{:S(2)}) collective-permute-start(bf16[2,256,2,128]{3,1,2,0:T(8,128)(2,1)} %get-tuple-element.260), channel_id=1, source_target_pairs={{0,4},{4,8},{8,12},{12,16},{16,20},{20,24},{24,28},{1,5},{5,9},{9,... | collective-permute-start | bytes 786440 | tf_op jit(solution)/shard_map/while/body/eval_jaxpr/ppermute | solution.py:17
  66.6 8.1 %collective-permute-done = bf16[2,256,2,128]{3,1,2,0:T(8,128)(2,1)S(1)} collective-permute-done((bf16[2,256,2,128]{3,1,2,0:T(8,128)(2,1)}, bf16[2,256,2,128]{3,1,2,0:T(8,128)(2,1)S(1)}, u32[]{:S(2)}, u32[]{:S(2)}) %collective-permute-start) | collective-permute-done | bytes 262176 | tf_op jit(solution)/shard_map/while/body/eval_jaxpr/ppermute | solution.py:17
  74.7 3.1 %conditional.2 = ((f32[2,8,256]{2,1,0:T(8,128)S(1)}, f32[2,8,256]{2,1,0:T(8,128)S(1)}, f32[2,8,256,128]{3,2,1,0:T(8,128)S(1)})) conditional(s32[]{:T(128)} %convert_element_type.38, (f32[2,8,256]{2,1,0:T(8,128)S(1)}, f32[2,8,256]{2,1,0:T(8,128)S(1)}, f32[2,8,256,128]{3,2,1,0:T(8,128)S(1)}) %tuple.43, (bf16[2,256,2,128]{3,1,2,0:T(8,128)(2,1)S(1)}, ...), branch_computations={%region_3.3_spmd, %region_4.6_spmd} | conditional | flops 546316288 | bytes 18350112 | solution.py:48
  76.2 1.6 %multiply_add_fusion = f32[2,8,256,128]{3,2,1,0:T(8,128)S(1)} fusion(f32[2,8,256,128]{3,2,1,0:T(8,128)S(1)} %get-tuple-element.146, f32[2,256,256,8]{2,1,3,0:T(8,128)S(1)} %get-tuple-element.186, f32[2,8,256]{2,1,0:T(8,128)S(1)} %max.2, f32[2,8,256]{2,1,0:T(8,128)S(1)} %get-tuple-element.184, bf16[2,256,2,128]{3,1,2,0:T(8,128)(2,1)S(1)} %get-tuple-element.143), kind=kOutput, calls=%fused_computation.6 | convolution fusion | flops 272629760 | bytes 8552448 | tf_op jit(solution)/shard_map/while/body/eval_jaxpr/cond/branch_1_fun/grqk,kgd->grqd/dot_general | solution.py:30
  78.5 1.3 %collective-permute-start = (bf16[2,256,2,128]{3,1,2,0:T(8,128)(2,1)}, bf16[2,256,2,128]{3,1,2,0:T(8,128)(2,1)S(1)}, u32[]{:S(2)}, u32[]{:S(2)}) collective-permute-start(bf16[2,256,2,128]{3,1,2,0:T(8,128)(2,1)} %get-tuple-element.260), channel_id=1, source_target_pairs={{0,4},{4,8},{8,12},{12,16},{16,20},{20,24},{24,28},{1,5},{5,9},{9,... | collective-permute-start | bytes 786440 | tf_op jit(solution)/shard_map/while/body/eval_jaxpr/ppermute | solution.py:17
  79.8 8.1 %collective-permute-done = bf16[2,256,2,128]{3,1,2,0:T(8,128)(2,1)S(1)} collective-permute-done((bf16[2,256,2,128]{3,1,2,0:T(8,128)(2,1)}, bf16[2,256,2,128]{3,1,2,0:T(8,128)(2,1)S(1)}, u32[]{:S(2)}, u32[]{:S(2)}) %collective-permute-start) | collective-permute-done | bytes 262176 | tf_op jit(solution)/shard_map/while/body/eval_jaxpr/ppermute | solution.py:17
  87.8 3.1 %conditional.2 = ((f32[2,8,256]{2,1,0:T(8,128)S(1)}, f32[2,8,256]{2,1,0:T(8,128)S(1)}, f32[2,8,256,128]{3,2,1,0:T(8,128)S(1)})) conditional(s32[]{:T(128)} %convert_element_type.38, (f32[2,8,256]{2,1,0:T(8,128)S(1)}, f32[2,8,256]{2,1,0:T(8,128)S(1)}, f32[2,8,256,128]{3,2,1,0:T(8,128)S(1)}) %tuple.43, (bf16[2,256,2,128]{3,1,2,0:T(8,128)(2,1)S(1)}, ...), branch_computations={%region_3.3_spmd, %region_4.6_spmd} | conditional | flops 546316288 | bytes 18350112 | solution.py:48
  89.3 1.6 %multiply_add_fusion = f32[2,8,256,128]{3,2,1,0:T(8,128)S(1)} fusion(f32[2,8,256,128]{3,2,1,0:T(8,128)S(1)} %get-tuple-element.146, f32[2,256,256,8]{2,1,3,0:T(8,128)S(1)} %get-tuple-element.186, f32[2,8,256]{2,1,0:T(8,128)S(1)} %max.2, f32[2,8,256]{2,1,0:T(8,128)S(1)} %get-tuple-element.184, bf16[2,256,2,128]{3,1,2,0:T(8,128)(2,1)S(1)} %get-tuple-element.143), kind=kOutput, calls=%fused_computation.6 | convolution fusion | flops 272629760 | bytes 8552448 | tf_op jit(solution)/shard_map/while/body/eval_jaxpr/cond/branch_1_fun/grqk,kgd->grqd/dot_general | solution.py:30
  93.0 8.1 %collective-permute-done = bf16[2,256,2,128]{3,1,2,0:T(8,128)(2,1)S(1)} collective-permute-done((bf16[2,256,2,128]{3,1,2,0:T(8,128)(2,1)}, bf16[2,256,2,128]{3,1,2,0:T(8,128)(2,1)S(1)}, u32[]{:S(2)}, u32[]{:S(2)}) %collective-permute-start) | collective-permute-done | bytes 262176 | tf_op jit(solution)/shard_map/while/body/eval_jaxpr/ppermute | solution.py:17
  101.0 3.1 %conditional.2 = ((f32[2,8,256]{2,1,0:T(8,128)S(1)}, f32[2,8,256]{2,1,0:T(8,128)S(1)}, f32[2,8,256,128]{3,2,1,0:T(8,128)S(1)})) conditional(s32[]{:T(128)} %convert_element_type.38, (f32[2,8,256]{2,1,0:T(8,128)S(1)}, f32[2,8,256]{2,1,0:T(8,128)S(1)}, f32[2,8,256,128]{3,2,1,0:T(8,128)S(1)}) %tuple.43, (bf16[2,256,2,128]{3,1,2,0:T(8,128)(2,1)S(1)}, ...), branch_computations={%region_3.3_spmd, %region_4.6_spmd} | conditional | flops 546316288 | bytes 18350112 | solution.py:48
  102.5 1.6 %multiply_add_fusion = f32[2,8,256,128]{3,2,1,0:T(8,128)S(1)} fusion(f32[2,8,256,128]{3,2,1,0:T(8,128)S(1)} %get-tuple-element.146, f32[2,256,256,8]{2,1,3,0:T(8,128)S(1)} %get-tuple-element.186, f32[2,8,256]{2,1,0:T(8,128)S(1)} %max.2, f32[2,8,256]{2,1,0:T(8,128)S(1)} %get-tuple-element.184, bf16[2,256,2,128]{3,1,2,0:T(8,128)(2,1)S(1)} %get-tuple-element.143), kind=kOutput, calls=%fused_computation.6 | convolution fusion | flops 272629760 | bytes 8552448 | tf_op jit(solution)/shard_map/while/body/eval_jaxpr/cond/branch_1_fun/grqk,kgd->grqd/dot_general | solution.py:30
  (59 shorter events, 22.9 us)
Async XLA Ops:
  2.6 3.8 %copy-start.1 = (bf16[256,2048]{0,1:T(8,128)(2,1)}, bf16[256,2048]{0,1:T(8,128)(2,1)S(1)}, u32[]{:S(2)}) copy-start(bf16[256,2048]{0,1:T(8,128)(2,1)S(1)} %copy.9) | copy-start | bytes 3145732
  3.5 1.9 %copy-start = (f32[2,256,256,8]{2,1,3,0:T(8,128)}, f32[2,256,256,8]{2,1,3,0:T(8,128)S(1)}, u32[]{:S(2)}) copy-start(f32[2,256,256,8]{2,1,3,0:T(8,128)S(1)} %get-tuple-element.190) | copy-start | bytes 12582916
  12.5 10.2 %collective-permute-start = (bf16[2,256,2,128]{3,1,2,0:T(8,128)(2,1)}, bf16[2,256,2,128]{3,1,2,0:T(8,128)(2,1)S(1)}, u32[]{:S(2)}, u32[]{:S(2)}) collective-permute-start(bf16[2,256,2,128]{3,1,2,0:T(8,128)(2,1)} %get-tuple-element.260), channel_id=1, source_target_pairs={{0,4},{4,8},{8,12},{12,16},{16,20},{20,24},{24,28},{1,5},{5,9},{9,... | collective-permute-start | bytes 786440 | tf_op jit(solution)/shard_map/while/body/eval_jaxpr/ppermute | solution.py:17
  26.5 9.3 %collective-permute-start = (bf16[2,256,2,128]{3,1,2,0:T(8,128)(2,1)}, bf16[2,256,2,128]{3,1,2,0:T(8,128)(2,1)S(1)}, u32[]{:S(2)}, u32[]{:S(2)}) collective-permute-start(bf16[2,256,2,128]{3,1,2,0:T(8,128)(2,1)} %get-tuple-element.260), channel_id=1, source_target_pairs={{0,4},{4,8},{8,12},{12,16},{16,20},{20,24},{24,28},{1,5},{5,9},{9,... | collective-permute-start | bytes 786440 | tf_op jit(solution)/shard_map/while/body/eval_jaxpr/ppermute | solution.py:17
  39.6 9.0 %collective-permute-start = (bf16[2,256,2,128]{3,1,2,0:T(8,128)(2,1)}, bf16[2,256,2,128]{3,1,2,0:T(8,128)(2,1)S(1)}, u32[]{:S(2)}, u32[]{:S(2)}) collective-permute-start(bf16[2,256,2,128]{3,1,2,0:T(8,128)(2,1)} %get-tuple-element.260), channel_id=1, source_target_pairs={{0,4},{4,8},{8,12},{12,16},{16,20},{20,24},{24,28},{1,5},{5,9},{9,... | collective-permute-start | bytes 786440 | tf_op jit(solution)/shard_map/while/body/eval_jaxpr/ppermute | solution.py:17
  52.4 9.1 %collective-permute-start = (bf16[2,256,2,128]{3,1,2,0:T(8,128)(2,1)}, bf16[2,256,2,128]{3,1,2,0:T(8,128)(2,1)S(1)}, u32[]{:S(2)}, u32[]{:S(2)}) collective-permute-start(bf16[2,256,2,128]{3,1,2,0:T(8,128)(2,1)} %get-tuple-element.260), channel_id=1, source_target_pairs={{0,4},{4,8},{8,12},{12,16},{16,20},{20,24},{24,28},{1,5},{5,9},{9,... | collective-permute-start | bytes 786440 | tf_op jit(solution)/shard_map/while/body/eval_jaxpr/ppermute | solution.py:17
  65.3 9.4 %collective-permute-start = (bf16[2,256,2,128]{3,1,2,0:T(8,128)(2,1)}, bf16[2,256,2,128]{3,1,2,0:T(8,128)(2,1)S(1)}, u32[]{:S(2)}, u32[]{:S(2)}) collective-permute-start(bf16[2,256,2,128]{3,1,2,0:T(8,128)(2,1)} %get-tuple-element.260), channel_id=1, source_target_pairs={{0,4},{4,8},{8,12},{12,16},{16,20},{20,24},{24,28},{1,5},{5,9},{9,... | collective-permute-start | bytes 786440 | tf_op jit(solution)/shard_map/while/body/eval_jaxpr/ppermute | solution.py:17
  78.5 9.4 %collective-permute-start = (bf16[2,256,2,128]{3,1,2,0:T(8,128)(2,1)}, bf16[2,256,2,128]{3,1,2,0:T(8,128)(2,1)S(1)}, u32[]{:S(2)}, u32[]{:S(2)}) collective-permute-start(bf16[2,256,2,128]{3,1,2,0:T(8,128)(2,1)} %get-tuple-element.260), channel_id=1, source_target_pairs={{0,4},{4,8},{8,12},{12,16},{16,20},{20,24},{24,28},{1,5},{5,9},{9,... | collective-permute-start | bytes 786440 | tf_op jit(solution)/shard_map/while/body/eval_jaxpr/ppermute | solution.py:17
  91.7 9.4 %collective-permute-start = (bf16[2,256,2,128]{3,1,2,0:T(8,128)(2,1)}, bf16[2,256,2,128]{3,1,2,0:T(8,128)(2,1)S(1)}, u32[]{:S(2)}, u32[]{:S(2)}) collective-permute-start(bf16[2,256,2,128]{3,1,2,0:T(8,128)(2,1)} %get-tuple-element.260), channel_id=1, source_target_pairs={{0,4},{4,8},{8,12},{12,16},{16,20},{20,24},{24,28},{1,5},{5,9},{9,... | collective-permute-start | bytes 786440 | tf_op jit(solution)/shard_map/while/body/eval_jaxpr/ppermute | solution.py:17
where the time goes:
time: 108 us; the launch traced here: 107 us
  waiting for transfers between devices  56.5 us (52%)
  matrix products  20.6 us (19%)
  local copies, waits for them, and re-layouts  13.8 us (13%)
  starting transfers between devices  8.97 us (8%)
  other arithmetic  6.95 us (6%)
    ppermute x7, waiting for transfers between devices, shifted(): lax.ppermute(value, axis, [(source, source + steps) for source in range(i...  56.5 us
    dot_general x8, matrix products, attend(): jnp.einsum('grqk,kgd->grqd', weights.astype(jnp.bfloat16), value_piece, p...  14.7 us
    ppermute x7, starting transfers between devices, shifted(): lax.ppermute(value, axis, [(source, source + steps) for source in range(i...  8.97 us
    reduce_sum x8, other arithmetic, attend(): totals = totals * factor + jnp.sum(weights, axis=-1)  6.04 us
    dot_general x8, matrix products, attend(): jnp.einsum('qgrd,kgd->grqk', grouped, key_piece, preferred_element_type=j...  5.86 us
    while x7, local copies, waits for them, and re-layouts  4.86 us
    unnamed x8, local copies, waits for them, and re-layouts  4.85 us
    while x2, local copies, waits for them, and re-layouts, circulate(): lax.fori_loop(1, turn_limit, cycle_turn, (acc_state, kv_pair))  2.44 us
  transfers between devices with their start and end apart: 7, of which 7 were waited for; matrix products, arithmetic and copies ran while one was open for 0% of the time, Pallas kernels for 0%

commit v1 on v0

v1 whole, which is shorter than its diff:
```python
import functools
import math

import jax
import jax.numpy as jnp
from jax import lax
from jax.experimental import pallas as pl
from jax.experimental.pallas import tpu as pltpu
from jax.sharding import PartitionSpec as P


H = 64
KVH = 8
HD = 128
BIG = 1e30
VMEM = pl.BlockSpec(memory_space=pltpu.VMEM)
NT = (((1,), (1,)), ((), ()))


def moved(value, target):
    ctx, head = lax.axis_size("ctx"), lax.axis_size("head")
    pairs = []
    for c in range(ctx):
        to = target(c)
        for h in range(head):
            if to is not None:
                pairs.append((c * head + h, to * head + h))
            elif head % 2 == 0:
                pairs.append((c * head + h, c * head + (h ^ 1)))
    return lax.ppermute(value, ("ctx", "head"), pairs)


def attend_kernel(q_ref, *refs, wanted, first, last, rep, heads, unroll, rb):
    kv_refs, refs = refs[: len(wanted)], refs[len(wanted) :]
    place = lax.axis_index("ctx")
    flags = [w(place) for w in wanted]
    if not first:
        m_in, a_in, *refs = refs
    if last:
        (o_ref,) = refs
    else:
        m_out, a_out = refs
    tok = q_ref.shape[0]
    scale = HD**-0.5 * math.log2(math.e)
    ones = jnp.ones((tok, HD), jnp.bfloat16)

    def one(h, r):
        rows = pl.ds(r * rb, rb)
        col = pl.ds(pl.multiple_of(h * HD, HD), HD)
        kcol = pl.multiple_of(h // rep * 2 * HD, 2 * HD)
        q = q_ref[rows, col]
        scores, shifts = [], []
        m_prev = m = None if first else m_in[h, rows]
        for i, kv in enumerate(kv_refs):
            k = kv[:, pl.ds(kcol, HD)]
            s = lax.dot_general(q, k, NT, preferred_element_type=jnp.float32) * scale
            if first:
                t = lax.broadcasted_iota(jnp.int32, s.shape, 0) + r * rb
                u = lax.broadcasted_iota(jnp.int32, s.shape, 1)
                s = jnp.where(t >= u, s, -BIG)
                bias = None
            else:
                bias = jnp.where(flags[i], 0.0, -BIG)
            top = jnp.max(s, axis=1, keepdims=True)
            top = jnp.broadcast_to(top if bias is None else top + bias, (rb, HD))
            m = top if m is None else jnp.maximum(m, top)
            scores.append(s)
            shifts.append(bias)
        acc = None
        for s, bias, kv in zip(scores, shifts, kv_refs):
            shift = m if bias is None else m - bias
            p = jnp.exp2(s - jnp.concatenate([shift] * (tok // HD), axis=1)).astype(jnp.bfloat16)
            v = jnp.concatenate([kv[:, pl.ds(kcol + HD, HD)], ones], axis=1)
            d = jnp.dot(p, v, preferred_element_type=jnp.float32)
            acc = d if acc is None else acc + d
        if not first:
            fade = jnp.exp2(m_prev - m)
            acc = acc + a_in[h, rows] * jnp.concatenate([fade, fade], axis=1)
        if last:
            o_ref[rows, col] = (acc[:, :HD] / acc[:, HD:]).astype(o_ref.dtype)
        else:
            m_out[h, rows] = m
            a_out[h, rows] = acc

    def work():
        def step(t, carry):
            for u in range(unroll):
                for r in range(tok // rb):
                    one(t * unroll + u, r)
            return carry

        lax.fori_loop(0, heads // unroll, step, 0)

    def finish():
        def step(h, carry):
            acc = a_in[h]
            o_ref[:, pl.ds(pl.multiple_of(h * HD, HD), HD)] = (acc[:, :HD] / acc[:, HD:]).astype(o_ref.dtype)
            return carry

        lax.fori_loop(0, heads, step, 0)

    if first:
        work()
        return
    live = functools.reduce(jnp.logical_or, flags)
    pl.when(live)(work)
    if last:
        pl.when(jnp.logical_not(live))(finish)


def attend(wanted, q, kvs, state, rep, last):
    tok, heads = q.shape[0], q.shape[1] // HD
    n, first = len(kvs), state is None
    held = [
        jax.ShapeDtypeStruct((heads, tok, HD), jnp.float32),
        jax.ShapeDtypeStruct((heads, tok, 2 * HD), jnp.float32),
    ]
    unroll = math.gcd(heads, 8)
    rb = math.gcd(tok, 128)
    return pl.pallas_call(
        functools.partial(attend_kernel, wanted=wanted, first=first, last=last, rep=rep, heads=heads, unroll=unroll, rb=rb),
        out_shape=jax.ShapeDtypeStruct(q.shape, q.dtype) if last else held,
        in_specs=[VMEM] * (1 + n + (0 if first else 2)),
        out_specs=VMEM if last else [VMEM, VMEM],
        input_output_aliases={} if first or last else {1 + n: 0, 2 + n: 1},
        compiler_params=pltpu.CompilerParams(vmem_limit_bytes=24 << 20),
        cost_estimate=pl.CostEstimate(
            flops=4 * tok * tok * HD * heads * n, transcendentals=tok * tok * heads * n, bytes_accessed=4 << 20
        ),
    )(q, *kvs, *(() if first else state))


def body(queries, keys, values):
    heads = queries.shape[1] // HD
    group = H // KVH
    kv_count = max(1, heads // group)
    rep = heads // kv_count
    first_col = lax.axis_index("head") * heads // group * HD
    k_own = lax.dynamic_slice_in_dim(keys, first_col, kv_count * HD, 1)
    v_own = lax.dynamic_slice_in_dim(values, first_col, kv_count * HD, 1)
    parts = []
    for g in range(kv_count):
        parts += [k_own[:, g * HD : (g + 1) * HD], v_own[:, g * HD : (g + 1) * HD]]
    own = jnp.concatenate(parts, axis=1)

    ctx = lax.axis_size("ctx")
    inner, outer = split(ctx)

    def down(k):
        def target(c):
            cz, cy = c // inner, c % inner
            if cz < k - 1:
                return None
            return (cz + 1 if cz < outer - 1 else k - 1) * inner + cy

        return target

    def across(k):
        return lambda c: c ^ 1 if c // inner >= k else None

    def below(k):
        return lambda place: place >= k * inner

    def odd(place):
        return lax.rem(place, 2) == 1

    line, pair = {}, {}

    def send_line(k, value):
        if k < outer:
            line[k] = moved(value, down(k))

    def send_pair(k, value):
        if inner == 2:
            pair[k] = moved(value, across(k))

    send_line(1, own)
    send_pair(0, own)
    state = attend([below(0)], queries, [own], None, rep, ctx == 1)
    for k in range(1, outer):
        send_line(k + 1, line[k])
        send_pair(k, line[k])
        came, wanted = [line[k]], [below(k)]
        if inner == 2:
            came.append(pair[k - 1])
            wanted.append(odd if k == 1 else below(k - 1))
        state = attend(wanted, queries, came, state, rep, inner == 1 and k == outer - 1)
    if inner == 2:
        wanted = [odd if outer == 1 else below(outer - 1)]
        state = attend(wanted, queries, [pair[outer - 1]], state, rep, True)
    return state


def split(ctx):
    inner = 2 if ctx % 2 == 0 else 1
    return inner, ctx // inner


def solution(mesh):
    return jax.shard_map(
        body,
        mesh=mesh,
        in_specs=(P("ctx", "head"), P("ctx", None), P("ctx", None)),
        out_specs=P("ctx", "head"),
        check_vma=False,
    )
```

time: 108 us -> 44.1 us (0.41)
  waiting for transfers between devices: 56.5 us -> 20.2 us
  matrix products: 20.6 us -> 0 us
  Pallas kernels: 0 us -> 16.6 us
  local copies, waits for them, and re-layouts: 13.8 us -> 2.18 us
  other arithmetic: 6.95 us -> 0.03 us
  starting transfers between devices: 8.97 us -> 4.88 us
    ppermute x7, waiting for transfers between devices: 56.5 us -> 20.2 us  [moved(): return lax.ppermute(value, ('ctx', 'head'), pairs)]
    dot_general x16 -> x0, matrix products: 20.6 us -> none  [the longest x8 14.7 us: attend(): jnp.einsum('grqk,kgd->grqd', weights.astype(jnp.bfloat16), value_piece, p...]
    pallas_call x0 -> x5, Pallas kernels: none -> 16.6 us  [attend(): pl.pallas_call(functools.partial(attend_kernel, wanted=wanted, first=firs...]
    while x9 -> x0, local copies, waits for them, and re-layouts: 7.3 us -> none
    reduce_sum x8 -> x0, other arithmetic: 6.04 us -> none  [attend(): totals = totals * factor + jnp.sum(weights, axis=-1)]
    ppermute x7, starting transfers between devices: 8.97 us -> 4.88 us  [moved(): return lax.ppermute(value, ('ctx', 'head'), pairs)]
    unnamed x8 -> x2, local copies, waits for them, and re-layouts: 4.85 us -> 1.22 us
  transfers between devices with their start and end apart: 7 -> 7, of which waited for: 7 -> 6; matrix products, arithmetic and copies ran while one was open for 0% -> 0% of each run, Pallas kernels for 0% -> 30%
where the time goes in v1:
time: 44.1 us; the launch traced here: 43.9 us
  waiting for transfers between devices  20.2 us (46%)
  Pallas kernels  16.6 us (38%)
  starting transfers between devices  4.88 us (11%)
  local copies, waits for them, and re-layouts  2.18 us (5%)
    ppermute x7, waiting for transfers between devices, moved(): return lax.ppermute(value, ('ctx', 'head'), pairs)  20.2 us
    pallas_call x5, Pallas kernels, attend(): pl.pallas_call(functools.partial(attend_kernel, wanted=wanted, first=firs...  16.6 us
    ppermute x7, starting transfers between devices, moved(): return lax.ppermute(value, ('ctx', 'head'), pairs)  4.88 us
    unnamed x2, local copies, waits for them, and re-layouts  1.22 us
    slice x1, local copies, waits for them, and re-layouts, body(): parts += [k_own[:, g * HD:(g + 1) * HD], v_own[:, g * HD:(g + 1) * HD]]  0.96 us
  transfers between devices with their start and end apart: 7, of which 6 were waited for; matrix products, arithmetic and copies ran while one was open for 0% of the time, Pallas kernels for 30%

profile of v1, /device:TPU:30, one launch (start us, length us, event | category | flops | bytes accessed | tf_op | source)
XLA Modules:
  0.0 43.9 jit_solution(15099878121199114949)
XLA Ops:
  0.0 1.0 %constant_dynamic-slice_fusion = (bf16[256,128]{1,0:T(8,128)(2,1)S(1)}, bf16[256,128]{1,0:T(8,128)(2,1)S(1)}, bf16[256,128]{1,0:T(8,128)(2,1)S(1)}, bf16[256,128]{1,0:T(8,128)(2,1)S(1)}) fusion(bf16[256,1024]{1,0:T(8,128)(2,1)} %param.5, s32[]{:T(128)S(6)} %select_n.10, s32[]{:T(128)S(6)} %add.6, bf16[256,1024]{1,0:T(8,128)(2,1)} %param.4), kind=kLoop, calls=%fused_computation.1 | loop fusion | bytes 524296 | tf_op jit(solution)/shard_map/slice | solution.py:143
  1.0 0.3 collective-permute-start
  1.3 7.8 %collective-permute-done.refs_0_ = bf16[256,512]{1,0:T(8,128)(2,1)S(1)} collective-permute-done((bf16[256,512]{1,0:T(8,128)(2,1)S(1)}, bf16[256,512]{1,0:T(8,128)(2,1)S(1)}, u32[]{:S(2)}, u32[]{:S(2)}) %collective-permute-start) | collective-permute-done | bytes 262176 | tf_op jit(solution)/shard_map/ppermute | solution.py:30
  9.1 0.3 collective-permute-start.1
  9.4 6.9 %collective-permute-done.1.refs_0_ = bf16[256,512]{1,0:T(8,128)(2,1)S(1)} collective-permute-done((bf16[256,512]{1,0:T(8,128)(2,1)S(1)}, bf16[256,512]{1,0:T(8,128)(2,1)S(1)}, u32[]{:S(2)}, u32[]{:S(2)}) %collective-permute-start.1) | collective-permute-done | bytes 262176 | tf_op jit(solution)/shard_map/ppermute | solution.py:30
  16.3 0.4 %collective-permute-start.2 = (bf16[256,512]{1,0:T(8,128)(2,1)S(1)}, bf16[256,512]{1,0:T(8,128)(2,1)S(1)}, u32[]{:S(2)}, u32[]{:S(2)}) collective-permute-start(bf16[256,512]{1,0:T(8,128)(2,1)S(1)} %collective-permute-done.1.refs_0_), channel_id=1, source_target_pairs={{0,1},{1,0},{2,3},{3,2},{4,5},{5,4},{6,7},{7,6},{8,9},{9,8},{10,11... | collective-permute-start | bytes 786440 | tf_op jit(solution)/shard_map/ppermute | solution.py:30
  16.7 0.5 %collective-permute-start.6 = (bf16[256,512]{1,0:T(8,128)(2,1)S(1)}, bf16[256,512]{1,0:T(8,128)(2,1)S(1)}, u32[]{:S(2)}, u32[]{:S(2)}) collective-permute-start(bf16[256,512]{1,0:T(8,128)(2,1)S(1)} %pad_maximum_fusion.refs_0_), channel_id=1, source_target_pairs={{0,4},{1,5},{2,6},{3,7},{4,0},{5,1},{6,2},{7,3},{8,12},{9,13},{10,... | collective-permute-start | bytes 786440 | tf_op jit(solution)/shard_map/ppermute | solution.py:30
  17.2 1.5 %collective-permute-start.5 = (bf16[256,512]{1,0:T(8,128)(2,1)S(1)}, bf16[256,512]{1,0:T(8,128)(2,1)S(1)}, u32[]{:S(2)}, u32[]{:S(2)}) collective-permute-start(bf16[256,512]{1,0:T(8,128)(2,1)S(1)} %collective-permute-done.refs_0_), channel_id=1, source_target_pairs={{0,1},{1,0},{2,3},{3,2},{4,5},{5,4},{6,7},{7,6},{8,12},{9,13},{10,... | collective-permute-start | bytes 786440 | tf_op jit(solution)/shard_map/ppermute | solution.py:30
  18.8 0.5 %collective-permute-start.4 = (bf16[256,512]{1,0:T(8,128)(2,1)S(1)}, bf16[256,512]{1,0:T(8,128)(2,1)S(1)}, u32[]{:S(2)}, u32[]{:S(2)}) collective-permute-start(bf16[256,512]{1,0:T(8,128)(2,1)S(1)} %collective-permute-done.1.refs_0_), channel_id=1, source_target_pairs={{0,1},{1,0},{2,3},{3,2},{4,5},{5,4},{6,7},{7,6},{8,9},{9,8},{10,11... | collective-permute-start | bytes 786440 | tf_op jit(solution)/shard_map/ppermute | solution.py:30
  19.3 0.0 copy-start
  19.3 1.2 %copy-done = bf16[256,2048]{1,0:T(8,128)(2,1)S(1)} copy-done((bf16[256,2048]{1,0:T(8,128)(2,1)S(1)}, bf16[256,2048]{1,0:T(8,128)(2,1)}, u32[]{:S(2)}) %copy-start) | copy-done | bytes 1048600
  20.5 1.9 %shard_map.37 = (f32[16,256,128]{2,1,0:T(8,128)S(1)}, f32[16,256,256]{2,1,0:T(8,128)S(1)}) custom-call(bf16[256,2048]{1,0:T(8,128)(2,1)S(1)} %copy-done, bf16[256,512]{1,0:T(8,128)(2,1)S(1)} %pad_maximum_fusion.refs_0_), custom_call_target="tpu_custom_call" | custom-call | flops 536870912 | bytes 4194304 | tf_op jit(solution)/shard_map/pallas_call | solution.py:120
  22.4 0.3 collective-permute-done.2.refs_0_
  22.7 1.3 %collective-permute-start.3 = (bf16[256,512]{1,0:T(8,128)(2,1)S(1)}, bf16[256,512]{1,0:T(8,128)(2,1)S(1)}, u32[]{:S(2)}, u32[]{:S(2)}) collective-permute-start(bf16[256,512]{1,0:T(8,128)(2,1)S(1)} %collective-permute-done.2.refs_0_), channel_id=1, source_target_pairs={{0,1},{1,0},{2,3},{3,2},{4,5},{5,4},{6,7},{7,6},{8,9},{9,8},{10,11... | collective-permute-start | bytes 786440 | tf_op jit(solution)/shard_map/ppermute | solution.py:30
  24.0 2.0 %collective-permute-done.6.refs_1_ = bf16[256,512]{1,0:T(8,128)(2,1)S(1)} collective-permute-done((bf16[256,512]{1,0:T(8,128)(2,1)S(1)}, bf16[256,512]{1,0:T(8,128)(2,1)S(1)}, u32[]{:S(2)}, u32[]{:S(2)}) %collective-permute-start.6) | collective-permute-done | bytes 262176 | tf_op jit(solution)/shard_map/ppermute | solution.py:30
  25.9 3.8 %shard_map.38 = (f32[16,256,128]{2,1,0:T(8,128)S(1)}, f32[16,256,256]{2,1,0:T(8,128)S(1)}) custom-call(bf16[256,2048]{1,0:T(8,128)(2,1)S(1)} %copy-done, bf16[256,512]{1,0:T(8,128)(2,1)S(1)} %collective-permute-done.refs_0_, bf16[256,512]{1,0:T(8,128)(2,1)S(1)} %collective-permute-done.6.refs_1_, ...), custom_call_target="tpu_custom_call", output_to_operand_aliasing={{0}: (3, {}), {1}: (4, {})} | custom-call | flops 1073741824 | bytes 4194304 | tf_op jit(solution)/shard_map/pallas_call | solution.py:120
  29.7 1.8 %collective-permute-done.5.refs_1_ = bf16[256,512]{1,0:T(8,128)(2,1)S(1)} collective-permute-done((bf16[256,512]{1,0:T(8,128)(2,1)S(1)}, bf16[256,512]{1,0:T(8,128)(2,1)S(1)}, u32[]{:S(2)}, u32[]{:S(2)}) %collective-permute-start.5) | collective-permute-done | bytes 262176 | tf_op jit(solution)/shard_map/ppermute | solution.py:30
  31.5 3.8 %shard_map.39 = (f32[16,256,128]{2,1,0:T(8,128)S(1)}, f32[16,256,256]{2,1,0:T(8,128)S(1)}) custom-call(bf16[256,2048]{1,0:T(8,128)(2,1)S(1)} %copy-done, bf16[256,512]{1,0:T(8,128)(2,1)S(1)} %collective-permute-done.1.refs_0_, bf16[256,512]{1,0:T(8,128)(2,1)S(1)} %collective-permute-done.5.refs_1_, ...), custom_call_target="tpu_custom_call", output_to_operand_aliasing={{0}: (3, {}), {1}: (4, {})} | custom-call | flops 1073741824 | bytes 4194304 | tf_op jit(solution)/shard_map/pallas_call | solution.py:120
  35.4 1.5 %collective-permute-done.4.refs_1_ = bf16[256,512]{1,0:T(8,128)(2,1)S(1)} collective-permute-done((bf16[256,512]{1,0:T(8,128)(2,1)S(1)}, bf16[256,512]{1,0:T(8,128)(2,1)S(1)}, u32[]{:S(2)}, u32[]{:S(2)}) %collective-permute-start.4) | collective-permute-done | bytes 262176 | tf_op jit(solution)/shard_map/ppermute | solution.py:30
  36.8 3.8 %shard_map.40 = (f32[16,256,128]{2,1,0:T(8,128)S(1)}, f32[16,256,256]{2,1,0:T(8,128)S(1)}) custom-call(bf16[256,2048]{1,0:T(8,128)(2,1)S(1)} %copy-done, bf16[256,512]{1,0:T(8,128)(2,1)S(1)} %collective-permute-done.2.refs_0_, bf16[256,512]{1,0:T(8,128)(2,1)S(1)} %collective-permute-done.4.refs_1_, ...), custom_call_target="tpu_custom_call", output_to_operand_aliasing={{0}: (3, {}), {1}: (4, {})} | custom-call | flops 1073741824 | bytes 4194304 | tf_op jit(solution)/shard_map/pallas_call | solution.py:120
  40.7 0.0 collective-permute-done.3.refs_0_
  40.7 3.2 %shard_map.41 = bf16[256,2048]{1,0:T(8,128)(2,1)} custom-call(bf16[256,2048]{1,0:T(8,128)(2,1)S(1)} %copy-done, bf16[256,512]{1,0:T(8,128)(2,1)S(1)} %collective-permute-done.3.refs_0_, f32[16,256,128]{2,1,0:T(8,128)S(1)} %get-tuple-element.19.refs_1_, f32[16,256,256]{2,1,0:T(8,128)S(1)} %get-tuple-element.20.refs_2_), custom_call_target="tpu_custom_call" | custom-call | flops 536870912 | bytes 4194304 | tf_op jit(solution)/shard_map/pallas_call | solution.py:120
  (1 shorter events, 0.0 us)
Async XLA Ops:
  1.0 8.1 %collective-permute-start = (bf16[256,512]{1,0:T(8,128)(2,1)S(1)}, bf16[256,512]{1,0:T(8,128)(2,1)S(1)}, u32[]{:S(2)}, u32[]{:S(2)}) collective-permute-start(bf16[256,512]{1,0:T(8,128)(2,1)S(1)} %pad_maximum_fusion.refs_0_), channel_id=1, source_target_pairs={{0,8},{1,9},{2,10},{3,11},{4,12},{5,13},{6,14},{7,15},{8,16},{9,17... | collective-permute-start | bytes 786440 | tf_op jit(solution)/shard_map/ppermute | solution.py:30
  9.1 7.2 %collective-permute-start.1 = (bf16[256,512]{1,0:T(8,128)(2,1)S(1)}, bf16[256,512]{1,0:T(8,128)(2,1)S(1)}, u32[]{:S(2)}, u32[]{:S(2)}) collective-permute-start(bf16[256,512]{1,0:T(8,128)(2,1)S(1)} %collective-permute-done.refs_0_), channel_id=1, source_target_pairs={{0,1},{1,0},{2,3},{3,2},{4,5},{5,4},{6,7},{7,6},{8,16},{9,17},{10,... | collective-permute-start | bytes 786440 | tf_op jit(solution)/shard_map/ppermute | solution.py:30
  16.3 6.4 %collective-permute-start.2 = (bf16[256,512]{1,0:T(8,128)(2,1)S(1)}, bf16[256,512]{1,0:T(8,128)(2,1)S(1)}, u32[]{:S(2)}, u32[]{:S(2)}) collective-permute-start(bf16[256,512]{1,0:T(8,128)(2,1)S(1)} %collective-permute-done.1.refs_0_), channel_id=1, source_target_pairs={{0,1},{1,0},{2,3},{3,2},{4,5},{5,4},{6,7},{7,6},{8,9},{9,8},{10,11... | collective-permute-start | bytes 786440 | tf_op jit(solution)/shard_map/ppermute | solution.py:30
  16.7 9.2 %collective-permute-start.6 = (bf16[256,512]{1,0:T(8,128)(2,1)S(1)}, bf16[256,512]{1,0:T(8,128)(2,1)S(1)}, u32[]{:S(2)}, u32[]{:S(2)}) collective-permute-start(bf16[256,512]{1,0:T(8,128)(2,1)S(1)} %pad_maximum_fusion.refs_0_), channel_id=1, source_target_pairs={{0,4},{1,5},{2,6},{3,7},{4,0},{5,1},{6,2},{7,3},{8,12},{9,13},{10,... | collective-permute-start | bytes 786440 | tf_op jit(solution)/shard_map/ppermute | solution.py:30
  17.2 14.3 %collective-permute-start.5 = (bf16[256,512]{1,0:T(8,128)(2,1)S(1)}, bf16[256,512]{1,0:T(8,128)(2,1)S(1)}, u32[]{:S(2)}, u32[]{:S(2)}) collective-permute-start(bf16[256,512]{1,0:T(8,128)(2,1)S(1)} %collective-permute-done.refs_0_), channel_id=1, source_target_pairs={{0,1},{1,0},{2,3},{3,2},{4,5},{5,4},{6,7},{7,6},{8,12},{9,13},{10,... | collective-permute-start | bytes 786440 | tf_op jit(solution)/shard_map/ppermute | solution.py:30
  18.8 18.1 %collective-permute-start.4 = (bf16[256,512]{1,0:T(8,128)(2,1)S(1)}, bf16[256,512]{1,0:T(8,128)(2,1)S(1)}, u32[]{:S(2)}, u32[]{:S(2)}) collective-permute-start(bf16[256,512]{1,0:T(8,128)(2,1)S(1)} %collective-permute-done.1.refs_0_), channel_id=1, source_target_pairs={{0,1},{1,0},{2,3},{3,2},{4,5},{5,4},{6,7},{7,6},{8,9},{9,8},{10,11... | collective-permute-start | bytes 786440 | tf_op jit(solution)/shard_map/ppermute | solution.py:30
  19.3 1.2 %copy-start = (bf16[256,2048]{1,0:T(8,128)(2,1)S(1)}, bf16[256,2048]{1,0:T(8,128)(2,1)}, u32[]{:S(2)}) copy-start(bf16[256,2048]{1,0:T(8,128)(2,1)} %q_ref.9) | copy-start | bytes 3145732
  22.7 18.0 %collective-permute-start.3 = (bf16[256,512]{1,0:T(8,128)(2,1)S(1)}, bf16[256,512]{1,0:T(8,128)(2,1)S(1)}, u32[]{:S(2)}, u32[]{:S(2)}) collective-permute-start(bf16[256,512]{1,0:T(8,128)(2,1)S(1)} %collective-permute-done.2.refs_0_), channel_id=1, source_target_pairs={{0,1},{1,0},{2,3},{3,2},{4,5},{5,4},{6,7},{7,6},{8,9},{9,8},{10,11... | collective-permute-start | bytes 786440 | tf_op jit(solution)/shard_map/ppermute | solution.py:30
